TPU v7x, 32 devices: a whole 2x2x4 slice. The times are simulated.
32 devices in a mesh: ma: 4 (over y, x), freq: 8 (over z, core).
Axes of the slice: x: 2, y: 2, z: 4, core: 2. Of those that a mesh axis runs over, the one named last changes fastest.
Arguments:
- m_table: int32 [8], P('ma'), may hold values from 0 to 1023, as said below
- retained_modes: int32 [8], P('ma'), may hold values from 128 to 512, as said below
- cycle_ids: int32 [32], P('ma'), may hold values from 1 to 2047, as said below
- kl_coeffs: bfloat16 [8, 4, 512], P('ma', None, 'freq'), may hold values from -6 to 6
- kl_vectors: bfloat16 [8, 512, 32, 512], P('ma', 'freq'), may hold values from -0.375 to 0.375
- beam_matrix: bfloat16 [8, 32, 1024, 512], P('ma', 'freq'), may hold values from -0.00390625 to 0.00390625
Outputs:
- sky_maps: float32 [32, 2, 32, 2048], P('ma', None, 'freq')
Inputs may be any that keep to these rules, and one draw needn't show every extreme that they name: `m_table`: all distinct; slots 2 q and 2 q + 1 hold two numbers that sum to 1023. `retained_modes`: some slot keeps all 512 modes. `cycle_ids`: all distinct.
All inputs are finite; a program needn't handle non-finite values.
Results may differ from a plain program's by a relative error of at most 0.01.
Values may be sent and summed in bfloat16 or wider, within the bound.
A program may use at most 64 MiB of HBM per device.

v0:
```python
import functools
import math

import jax
import jax.numpy as jnp
from jax import lax
from jax.experimental import pallas as pl
from jax.experimental.pallas import tpu as pltpu
from jax.sharding import PartitionSpec as P

NPHI = 2048
NSIDE = 512
SEGMENTS = 8
MESH = pl.DeviceIdType.MESH
F32 = jnp.float32
BF16 = jnp.bfloat16
BIG = 2.0**30
SHRINK = 2.0**-60


def cycle_angles(cycle_numbers):
    cycle_float = cycle_numbers.astype(F32)
    nside_float = float(NSIDE)
    from_pole = jnp.minimum(cycle_float, 4.0 * nside_float - cycle_float)
    hemisphere = jnp.where(cycle_float <= 2.0 * nside_float, 1.0, -1.0)
    polar_part = from_pole * from_pole / (3.0 * nside_float * nside_float)
    polar_sin = from_pole / (math.sqrt(3.0) * nside_float) * jnp.sqrt(2.0 - polar_part)
    latitude_cosine = 4.0 / 3.0 - 2.0 * from_pole / (3.0 * nside_float)
    latitude_sine = jnp.sqrt(jnp.maximum(1.0 - latitude_cosine * latitude_cosine, 0.25))
    in_cap = from_pole < nside_float
    cos_theta = hemisphere * jnp.where(in_cap, 1.0 - polar_part, latitude_cosine)
    sin_theta = jnp.where(in_cap, polar_sin, latitude_sine)
    return (cos_theta, sin_theta)


def central_ratio(m_float):
    shifted = m_float + 0.25
    inverse = 1.0 / (shifted * shifted)
    series = 1.0 + inverse * (-1.0 / 64.0 + inverse * (21.0 / 8192.0))
    ratio = series / jnp.sqrt(math.pi * shifted)
    exact = 1.0
    for m in range(8):
        ratio = jnp.where(m_float == float(m), exact, ratio)
        exact = exact * (2 * m + 1) / (2 * m + 2)
    return ratio


def gather_kernel(
    n_ma, n_freq, m_ref, kept_ref, cyc_ref, coef_ref, vec_hbm, ints_out, svd_out,
    ints, ints_send, vec, send, recv, vec_sem, isend_sem, irecv_sem, send_sem, recv_sem,
):
    slots, quads, modes = coef_ref.shape
    channels, depth = vec_hbm.shape[2], vec_hbm.shape[3]
    n_cyc = cyc_ref.shape[0]
    rows = quads * channels
    block_rows = rows // n_freq
    ma, fr = lax.axis_index("ma"), lax.axis_index("freq")
    pieces = [
        pltpu.make_async_copy(vec_hbm.at[s], vec.at[s], vec_sem.at[s]) for s in range(slots)
    ]
    for piece in pieces:
        piece.start()
    barrier = pltpu.get_barrier_semaphore()
    for k in range(1, n_ma):
        pl.semaphore_signal(
            barrier, inc=1, device_id=(lax.rem(ma + k, n_ma), fr), device_id_type=MESH
        )
    for k in range(1, n_freq):
        pl.semaphore_signal(
            barrier, inc=1, device_id=(ma, lax.rem(fr + k, n_freq)), device_id_type=MESH
        )
    pack_shape = ints_send.shape
    lane = lax.broadcasted_iota(jnp.int32, pack_shape, 1)
    line = lax.broadcasted_iota(jnp.int32, pack_shape, 0)
    packed = jnp.zeros(pack_shape, jnp.int32)
    for i in range(n_cyc):
        here = (line == 0) & (lane % (n_cyc * n_ma) == ma * n_cyc + i)
        packed = jnp.where(here, cyc_ref[i], packed)
    for s in range(slots):
        packed = jnp.where((line == 1) & (lane == ma * slots + s), m_ref[s], packed)
    ints_send[...] = packed
    wide = modes * channels
    row = lax.broadcasted_iota(jnp.int32, (rows, wide), 0)
    column = lax.broadcasted_iota(jnp.int32, (rows, wide), 1)
    same_channel = row // quads == column % channels
    spread = (
        lax.broadcasted_iota(jnp.int32, (modes, wide), 1) // channels
        == lax.broadcasted_iota(jnp.int32, (modes, wide), 0)
    )
    spread = jnp.where(spread, 1.0, 0.0).astype(BF16)
    repeat = (
        lax.broadcasted_iota(jnp.int32, (rows, quads), 0) % quads
        == lax.broadcasted_iota(jnp.int32, (rows, quads), 1)
    )
    repeat = jnp.where(repeat, 1.0, 0.0).astype(BF16)
    mode = fr * modes + lax.broadcasted_iota(jnp.int32, (quads, modes), 1)
    pl.semaphore_wait(barrier, n_ma - 1 + n_freq - 1)
    int_copies = []
    for k in range(1, n_ma):
        copy = pltpu.make_async_remote_copy(
            src_ref=ints_send, dst_ref=ints.at[k], send_sem=isend_sem.at[k],
            recv_sem=irecv_sem.at[k], device_id=(lax.rem(ma + k, n_ma), fr), device_id_type=MESH,
        )
        copy.start()
        int_copies.append(copy)
    for s in range(slots):
        masked = jnp.where(mode < kept_ref[s], coef_ref[s].astype(F32), 0.0).astype(BF16)
        tall = jnp.dot(repeat, masked, preferred_element_type=F32).astype(BF16)
        full = jnp.dot(tall, spread, preferred_element_type=F32)
        weights = jnp.where(same_channel, full, 0.0).astype(BF16)
        pieces[s].wait()
        flat = vec[s].reshape(wide, depth)
        part = jnp.dot(weights, flat, preferred_element_type=F32).astype(BF16)
        for f in range(n_freq):
            send[f, s] = part[f * block_rows : (f + 1) * block_rows]
    copies = []
    for k in range(1, n_freq):
        to = lax.rem(fr + k, n_freq)
        copy = pltpu.make_async_remote_copy(
            src_ref=send.at[to], dst_ref=recv.at[k], send_sem=send_sem.at[k],
            recv_sem=recv_sem.at[k], device_id=(ma, to), device_id_type=MESH,
        )
        copy.start()
        copies.append(copy)
    for copy in int_copies:
        copy.wait()
    for k in range(1, n_ma):
        packed = packed + ints[k]
    ints_out[...] = packed
    total = send[fr].astype(F32)
    for k in range(1, n_freq):
        copies[k - 1].wait()
        total = total + recv[k].astype(F32)
    svd_out[...] = total.astype(BF16)


def gather_call(n_ma, n_freq, m_table, retained_modes, cycle_ids, kl_coeffs, kl_vectors):
    slots, quads, modes = kl_coeffs.shape
    channels, depth = kl_vectors.shape[2:]
    block_rows = quads * channels // n_freq
    wide = 2 * slots * n_ma * cycle_ids.shape[0]
    smem = pl.BlockSpec(memory_space=pltpu.SMEM)
    vmem = pl.BlockSpec(memory_space=pltpu.VMEM)
    return pl.pallas_call(
        functools.partial(gather_kernel, n_ma, n_freq),
        out_shape=(
            jax.ShapeDtypeStruct((8, wide), jnp.int32),
            jax.ShapeDtypeStruct((slots, block_rows, depth), BF16),
        ),
        in_specs=[smem, smem, smem, vmem, pl.BlockSpec(memory_space=pl.ANY)],
        out_specs=(vmem, vmem),
        scratch_shapes=[
            pltpu.VMEM((n_ma, 8, wide), jnp.int32),
            pltpu.VMEM((8, wide), jnp.int32),
            pltpu.VMEM(kl_vectors.shape, BF16),
            pltpu.VMEM((n_freq, slots, block_rows, depth), BF16),
            pltpu.VMEM((n_freq, slots, block_rows, depth), BF16),
            pltpu.SemaphoreType.DMA((slots,)),
            pltpu.SemaphoreType.DMA((n_ma,)),
            pltpu.SemaphoreType.DMA((n_ma,)),
            pltpu.SemaphoreType.DMA((n_freq,)),
            pltpu.SemaphoreType.DMA((n_freq,)),
        ],
        compiler_params=pltpu.CompilerParams(collective_id=0, has_side_effects=True),
        name="gather_svd",
    )(m_table, retained_modes, cycle_ids, kl_coeffs, kl_vectors)


def lane_values(m_ref, ints_ref, slots, cycles):
    cos_theta, sin_theta = cycle_angles(ints_ref[0:1, :])
    slot = lax.broadcasted_iota(jnp.int32, cos_theta.shape, 1) // cycles % slots
    m = jnp.zeros(cos_theta.shape, F32)
    for s in range(slots):
        m = jnp.where(slot == s, m_ref[s].astype(F32), m)
    mantissa = jnp.sqrt((2.0 * m + 1.0) * (1.0 / (4.0 * math.pi)) * central_ratio(m))
    power = m * (jnp.log(sin_theta) * (1.0 / math.log(2.0)))
    whole = jnp.floor(power)
    return (m, cos_theta, mantissa * jnp.exp2(power - whole), whole)


def legendre_into(values, rows_ref, exps_ref, leg_ref):
    length, _, wide = rows_ref.shape
    half = wide // 2
    shape = (SEGMENTS, wide)
    m_row, c_row, mantissa, whole = values
    m = jnp.broadcast_to(m_row, shape)
    c = jnp.broadcast_to(c_row, shape)
    first = lax.broadcasted_iota(jnp.int32, shape, 1) < half
    base = (lax.broadcasted_iota(jnp.int32, shape, 0) * length).astype(F32)

    def ratio(degree):
        after = degree - m > 0.5
        y = (degree - m) * (degree + m) / ((2.0 * degree - 1.0) * (2.0 * degree + 1.0))
        y = jnp.where(after, y, 1.0)
        a = lax.rsqrt(y)
        a = a * (1.5 - 0.5 * y * a * a)
        return (after, a, jnp.where(after, y * a, 0.0))

    steps = 4

    def body(i, state):
        p1, p2, e, root = state
        for u in range(steps):
            j = i * steps + u
            after, a, next_root = ratio(base + j.astype(F32))
            p = jnp.where(after, a * c, 1.0) * p1 - a * root * p2
            p1, p2, root = p, p1, next_root
            rows_ref[j] = p
            exps_ref[j] = e
        large = jnp.maximum(jnp.abs(p1), jnp.abs(p2)) > BIG
        scale = jnp.where(large, SHRINK, 1.0)
        return (p1 * scale, p2 * scale, jnp.where(large, e + 60.0, e), root)

    one = jnp.where(first, 1.0, 0.0)
    lax.fori_loop(
        0, length // steps, body,
        (one, 1.0 - one, jnp.zeros(shape, F32), ratio(base - 1.0)[2]), unroll=2,
    )
    last, last_e = rows_ref[length - 1], exps_ref[length - 1]
    before, before_e = rows_ref[length - 2], exps_ref[length - 2]
    top = jnp.maximum(last_e, pltpu.roll(last_e, half, 1))
    last = last * jnp.exp2(jnp.maximum(last_e - top, -126.0))
    before = before * jnp.exp2(jnp.maximum(before_e - top, -126.0))
    x = jnp.where(first[0:1], mantissa, 0.0)
    x_e = whole
    starts, starts_e = [], []
    for s in range(SEGMENTS):
        starts.append(x)
        starts_e.append(x_e)
        if s < SEGMENTS - 1:
            t1, t2 = x * last[s : s + 1], x * before[s : s + 1]
            t1, t2 = t1 + pltpu.roll(t1, half, 1), t2 + pltpu.roll(t2, half, 1)
            size = jnp.maximum(jnp.abs(t1), jnp.abs(t2))
            x = jnp.where(first[0:1], t1, t2)
            large, small = size > BIG, size < 1.0 / BIG
            x = x * jnp.where(large, SHRINK, jnp.where(small, 1.0 / SHRINK, 1.0))
            x_e = x_e + top[s : s + 1] + jnp.where(large, 60.0, jnp.where(small, -60.0, 0.0))
    for s in range(SEGMENTS):
        exponent = exps_ref[:, s, :] + starts_e[s]
        low = jnp.floor(exponent * 0.5)
        degree = (
            s * length + lax.broadcasted_iota(jnp.int32, (length, wide), 0)
        ).astype(F32)
        value = rows_ref[:, s, :] * jnp.exp2(jnp.maximum(low, -126.0)) * starts[s]
        value = value * jnp.exp2(jnp.maximum(exponent - low, -126.0))
        value = jnp.where(degree >= m_row, value, 0.0)
        turned = value.T
        leg_ref[:, s * length : (s + 1) * length] = (turned[:half] + turned[half:]).astype(BF16)


def synth_kernel(m_ref, ints_ref, svd_ref, beam_ref, out_ref, rows_ref, exps_ref, leg_ref):
    s, c = pl.program_id(0), pl.program_id(1)
    slots, block_rows, depth = svd_ref.shape
    n_ch = pl.num_programs(1)
    cycles = leg_ref.shape[0] // slots
    quads = 4

    @pl.when((s == 0) & (c == 0))
    def _():
        values = lane_values(m_ref, ints_ref, slots, cycles)
        legendre_into(values, rows_ref, exps_ref, leg_ref)
        out_ref[...] = jnp.zeros_like(out_ref)

    leg = leg_ref[pl.ds(pl.multiple_of(s * cycles, cycles), cycles), :]
    table = jnp.dot(leg, beam_ref[0, 0], preferred_element_type=F32).astype(BF16)
    svd = svd_ref[...].reshape(slots * block_rows, depth)
    svd = jnp.concatenate([svd, jnp.zeros((128 - slots * block_rows, depth), BF16)], axis=0)
    modes = lax.dot_general(
        table, svd, (((1,), (1,)), ((), ())), preferred_element_type=F32
    )
    group = lax.broadcasted_iota(jnp.int32, modes.shape, 1) // quads
    out_ref[...] += jnp.where(group == s * n_ch + c, modes, 0.0)


def synth_call(m_table, ints, svd, beam_matrix, cycles):
    slots, channels, length, depth = beam_matrix.shape
    wide = ints.shape[1]
    return pl.pallas_call(
        synth_kernel,
        grid=(slots, channels),
        out_shape=jax.ShapeDtypeStruct((cycles, 128), F32),
        in_specs=[
            pl.BlockSpec(memory_space=pltpu.SMEM),
            pl.BlockSpec(ints.shape, lambda s, c: (0, 0)),
            pl.BlockSpec(svd.shape, lambda s, c: (0, 0, 0)),
            pl.BlockSpec((1, 1, length, depth), lambda s, c: (s, c, 0, 0)),
        ],
        out_specs=pl.BlockSpec((cycles, 128), lambda s, c: (0, 0)),
        scratch_shapes=[
            pltpu.VMEM((length // SEGMENTS, SEGMENTS, wide), F32),
            pltpu.VMEM((length // SEGMENTS, SEGMENTS, wide), F32),
            pltpu.VMEM((slots * cycles, length), BF16),
        ],
        name="synth_cycles",
    )(m_table, ints, svd, beam_matrix)


def turn_cosine(turns):
    half = NPHI // 2
    u = NPHI // 4 - jnp.abs((turns & (NPHI - 1)) - half)
    x = u.astype(F32) * (2.0 * math.pi / NPHI)
    z = x * x
    series = -1.0 / 39916800.0
    for coefficient in (1.0 / 362880.0, -1.0 / 5040.0, 1.0 / 120.0, -1.0 / 6.0, 1.0):
        series = coefficient + z * series
    return -x * series


def swap_kernel(n_ma, slots, channels, ints_ref, in_ref, out_ref, recv, send_sem, recv_sem):
    ma, fr = lax.axis_index("ma"), lax.axis_index("freq")
    mine, lanes = recv.shape[1:]
    barrier = pltpu.get_barrier_semaphore()
    for k in range(1, n_ma):
        pl.semaphore_signal(
            barrier, inc=1, device_id=(lax.rem(ma + k, n_ma), fr), device_id_type=MESH
        )
    pl.semaphore_wait(barrier, n_ma - 1)
    copies = []
    for k in range(1, n_ma):
        to = lax.rem(ma + k, n_ma)
        copy = pltpu.make_async_remote_copy(
            src_ref=in_ref.at[pl.ds(pl.multiple_of(to * mine, mine), mine)],
            dst_ref=recv.at[k], send_sem=send_sem.at[k], recv_sem=recv_sem.at[k],
            device_id=(to, fr), device_id_type=MESH,
        )
        copy.start()
        copies.append(copy)
    depth = n_ma * slots * 2
    line = lax.broadcasted_iota(jnp.int32, (depth, NPHI), 0)
    time = lax.broadcasted_iota(jnp.int32, (depth, NPHI), 1)
    m = jnp.zeros((depth, NPHI), jnp.int32)
    for a in range(n_ma):
        for s in range(slots):
            m = jnp.where(line // 2 == a * slots + s, ints_ref[1, a * slots + s], m)
    table = turn_cosine(m * time + (line % 2) * (NPHI // 4))
    table = (jnp.where(m == 0, 1.0, 2.0) * table).astype(BF16)
    rows = mine * 2 * channels
    row = lax.broadcasted_iota(jnp.int32, (rows, lanes), 0)
    lane = lax.broadcasted_iota(jnp.int32, (rows, lanes), 1)
    wanted = (lane // 4 % channels == row % channels) & (lane % 4 // 2 == row // channels % 2)
    wanted = wanted & (lane < slots * channels * 4)
    from_lane = lax.broadcasted_iota(jnp.int32, (lanes, depth), 0)
    to_lane = lax.broadcasted_iota(jnp.int32, (lanes, depth), 1)
    from_lane = from_lane // (4 * channels) * 2 + from_lane % 2
    left = jnp.zeros((rows, depth), F32)
    for k in range(n_ma):
        if k == 0:
            block = in_ref[pl.ds(pl.multiple_of(ma * mine, mine), mine)]
        else:
            copies[k - 1].wait()
            block = recv[k]
        spread = jnp.broadcast_to(block[:, None, :], (mine, 2 * channels, lanes))
        spread = jnp.where(wanted, spread.reshape(rows, lanes), 0.0).astype(BF16)
        source = lax.rem(ma - k + n_ma, n_ma)
        pick = jnp.where(to_lane == from_lane + source * (2 * slots), 1.0, 0.0).astype(BF16)
        left = left + jnp.dot(spread, pick, preferred_element_type=F32)
    out_ref[...] = jnp.dot(left.astype(BF16), table, preferred_element_type=F32)


def swap_call(n_ma, slots, channels, ints, modes):
    mine = modes.shape[0] // n_ma
    vmem = pl.BlockSpec(memory_space=pltpu.VMEM)
    return pl.pallas_call(
        functools.partial(swap_kernel, n_ma, slots, channels),
        out_shape=jax.ShapeDtypeStruct((mine * 2 * channels, NPHI), F32),
        in_specs=[pl.BlockSpec(memory_space=pltpu.SMEM), vmem],
        out_specs=vmem,
        scratch_shapes=[
            pltpu.VMEM((n_ma, mine, 128), F32),
            pltpu.SemaphoreType.DMA((n_ma,)),
            pltpu.SemaphoreType.DMA((n_ma,)),
        ],
        compiler_params=pltpu.CompilerParams(collective_id=1, has_side_effects=True),
        name="swap_cycles",
    )(ints, modes)


def local(n_ma, n_freq, m_table, retained_modes, cycle_ids, kl_coeffs, kl_vectors, beam_matrix):
    slots, n_cyc = m_table.shape[0], cycle_ids.shape[0]
    channels = beam_matrix.shape[1]
    ints, svd = gather_call(
        n_ma, n_freq, m_table, retained_modes, cycle_ids, kl_coeffs, kl_vectors
    )
    modes = synth_call(m_table, ints, svd, beam_matrix, n_cyc * n_ma)
    sky = swap_call(n_ma, slots, channels, ints, modes)
    return sky.reshape(n_cyc, 2, channels, NPHI)


def solution(mesh):
    placed = (
        P("ma"),
        P("ma"),
        P("ma"),
        P("ma", None, "freq"),
        P("ma", "freq", None, None),
        P("ma", "freq", None, None),
    )
    return jax.shard_map(
        functools.partial(local, mesh.shape["ma"], mesh.shape["freq"]),
        mesh=mesh, in_specs=placed, out_specs=P("ma", None, "freq", None), check_vma=False,
    )
```

profile of v0, /device:TPU:0, one launch (start us, length us, event | category | flops | bytes accessed | tf_op | source)
XLA Modules:
  0.0 32.5 jit_solution(14300871869026058304)
XLA Ops:
  0.0 14.2 %gather_svd.1 = (s32[8,128]{1,0:T(8,128)}, bf16[2,16,512]{2,1,0:T(8,128)(2,1)}) custom-call(s32[2]{0:T(128)} %m_ref.3, s32[2]{0:T(128)} %kept_ref.1, s32[8]{0:T(128)} %cyc_ref.1, bf16[2,4,64]{2,1,0:T(4,128)(2,1)} %coef_ref.1, bf16[2,64,32,512]{3,2,1,0:T(8,128)(2,1)} %vec_hbm.1), custom_call_target="tpu_custom_call" | custom-call | tf_op jit(solution)/shard_map/gather_svd/pallas_call | solution.py:144
  14.2 9.7 %synth_cycles.1.in_ref = f32[32,128]{1,0:T(8,128)} custom-call(s32[2]{0:T(128)} %m_ref.3, s32[8,128]{1,0:T(8,128)} %get-tuple-element.7.ints_ref, bf16[2,16,512]{2,1,0:T(8,128)(2,1)} %get-tuple-element.8.svd_ref, bf16[2,4,1024,512]{3,2,1,0:T(8,128)(2,1)} %beam_ref.1), custom_call_target="tpu_custom_call" | custom-call | tf_op jit(solution)/shard_map/synth_cycles/pallas_call | solution.py:278
  23.9 6.6 %swap_cycles.1 = f32[64,2048]{1,0:T(8,128)} custom-call(s32[8,128]{1,0:T(8,128)} %get-tuple-element.7.ints_ref, f32[32,128]{1,0:T(8,128)} %synth_cycles.1.in_ref), custom_call_target="tpu_custom_call" | custom-call | tf_op jit(solution)/shard_map/swap_cycles/pallas_call | solution.py:363
  30.5 2.0 %reshape.3 = f32[8,2,4,2048]{3,2,1,0:T(4,128)} reshape(f32[64,2048]{1,0:T(8,128)} %swap_cycles.1) | data formatting | bytes 1048576 | tf_op jit(solution)/shard_map/reshape | solution.py:386
where the time goes:
time: 32.8 us; the launch traced here: 32.5 us
  Pallas kernels  30.5 us (93%)
  local copies, waits for them, and re-layouts  1.98 us (6%)
    pallas_call x1, Pallas kernels, gather_call(): pl.pallas_call(functools.partial(gather_kernel, n_ma, n_freq), out_shape=...  14.2 us
    pallas_call x1, Pallas kernels, synth_call(): pl.pallas_call(synth_kernel, grid=(slots, channels), out_shape=jax.ShapeD...  9.67 us
    pallas_call x1, Pallas kernels, swap_call(): pl.pallas_call(functools.partial(swap_kernel, n_ma, slots, channels), out...  6.56 us
    reshape x1, local copies, waits for them, and re-layouts, local(): return sky.reshape(n_cyc, 2, channels, NPHI)  1.98 us

commit v1 on v0

v1 whole, which is shorter than its diff:
```python
import functools
import math

import jax
import jax.numpy as jnp
from jax import lax
from jax.experimental import pallas as pl
from jax.experimental.pallas import tpu as pltpu
from jax.sharding import PartitionSpec as P

NPHI = 2048
NSIDE = 512
STEPS = 32
LANES = 128
MESH = pl.DeviceIdType.MESH
F32 = jnp.float32
BF16 = jnp.bfloat16
BIG = 2.0**30
SHRINK = 2.0**-60


def cycle_angles(cycle_numbers):
    cycle_float = cycle_numbers.astype(F32)
    nside_float = float(NSIDE)
    from_pole = jnp.minimum(cycle_float, 4.0 * nside_float - cycle_float)
    hemisphere = jnp.where(cycle_float <= 2.0 * nside_float, 1.0, -1.0)
    polar_part = from_pole * from_pole / (3.0 * nside_float * nside_float)
    polar_sin = from_pole / (math.sqrt(3.0) * nside_float) * jnp.sqrt(2.0 - polar_part)
    latitude_cosine = 4.0 / 3.0 - 2.0 * from_pole / (3.0 * nside_float)
    latitude_sine = jnp.sqrt(jnp.maximum(1.0 - latitude_cosine * latitude_cosine, 0.25))
    in_cap = from_pole < nside_float
    cos_theta = hemisphere * jnp.where(in_cap, 1.0 - polar_part, latitude_cosine)
    sin_theta = jnp.where(in_cap, polar_sin, latitude_sine)
    return (cos_theta, sin_theta)


def central_ratio(m_float):
    shifted = m_float + 0.25
    inverse = 1.0 / (shifted * shifted)
    series = 1.0 + inverse * (-1.0 / 64.0 + inverse * (21.0 / 8192.0))
    ratio = series / jnp.sqrt(math.pi * shifted)
    exact = 1.0
    for m in range(8):
        ratio = jnp.where(m_float == float(m), exact, ratio)
        exact = exact * (2 * m + 1) / (2 * m + 2)
    return ratio


def start_values(m, sin_theta):
    mantissa = jnp.sqrt((2.0 * m + 1.0) * (1.0 / (4.0 * math.pi)) * central_ratio(m))
    power = m * (jnp.log(sin_theta) * (1.0 / math.log(2.0)))
    whole = jnp.floor(power)
    return (mantissa * jnp.exp2(power - whole), whole)


def turn_cosine(turns):
    half = NPHI // 2
    u = NPHI // 4 - jnp.abs((turns & (NPHI - 1)) - half)
    x = u.astype(F32) * (2.0 * math.pi / NPHI)
    z = x * x
    series = -1.0 / 39916800.0
    for coefficient in (1.0 / 362880.0, -1.0 / 5040.0, 1.0 / 120.0, -1.0 / 6.0, 1.0):
        series = coefficient + z * series
    return -x * series


def rescaled(values, exponent):
    size = functools.reduce(jnp.maximum, [jnp.abs(v) for v in values])
    large, small = size > BIG, size < 1.0 / BIG
    scale = jnp.where(large, SHRINK, jnp.where(small, 1.0 / SHRINK, 1.0))
    shift = jnp.where(large, 60.0, jnp.where(small, -60.0, 0.0))
    return [v * scale for v in values], exponent + shift


def product(after, before, exponent):
    a, b, c, d = after
    p, q, r, s = before
    return rescaled([a * p + b * r, a * q + b * s, c * p + d * r, c * q + d * s], exponent)


def legendre_into(m_values, cos_theta, sin_theta, cycles, length, u_ref, v_ref, leg_ref):
    slots = len(m_values)
    parts = LANES // cycles
    blocks = length // (STEPS * 8 * parts)
    assert blocks == 1 or parts == 1
    shape = (8, LANES)
    sub = lax.broadcasted_iota(jnp.int32, shape, 0)
    part = lax.broadcasted_iota(jnp.int32, shape, 1) // cycles
    c = jnp.broadcast_to(cos_theta, shape)
    bases = [
        (((b * parts + part) * 8 + sub) * STEPS).astype(F32)
        for _ in range(slots) for b in range(blocks)
    ]
    ms = [m_values[s] for s in range(slots) for _ in range(blocks)]

    def ratio(degree, m):
        after = degree - m > 0.5
        y = (degree - m) * (degree + m) / ((2.0 * degree - 1.0) * (2.0 * degree + 1.0))
        y = jnp.where(after, y, 1.0)
        a = lax.rsqrt(y)
        a = a * (1.5 - 0.5 * y * a * a)
        return (after, a, jnp.where(after, y * a, 0.0))

    unroll = 8

    def body(i, state):
        for k in range(unroll):
            t = i * unroll + k
            later = []
            for j, (u1, u2, v1, v2, root) in enumerate(state):
                after, a, next_root = ratio(bases[j] + t.astype(F32), ms[j])
                alpha = jnp.where(after, a * c, 1.0)
                beta = a * root
                u = alpha * u1 - beta * u2
                v = alpha * v1 - beta * v2
                u_ref[j, t] = u
                v_ref[j, t] = v
                later.append((u, u1, v, v1, next_root))
            state = tuple(later)
        return state

    one, zero = jnp.ones(shape, F32), jnp.zeros(shape, F32)
    state = tuple(
        (one, zero, zero, one, ratio(base - 1.0, m)[2]) for base, m in zip(bases, ms)
    )
    state = lax.fori_loop(0, STEPS // unroll, body, state)
    log_starts = [start_values(jnp.full((1, LANES), m, F32), sin_theta) for m in m_values]
    for j, (u1, u2, v1, v2, _) in enumerate(state):
        s, b = j // blocks, j % blocks
        matrix, exponent = rescaled([u1, v1, u2, v2], zero)
        matrix, exponent = rescaled(matrix, exponent)
        for d in (1, 2, 4):
            low = sub < d
            before = [
                jnp.where(low, unit, pltpu.roll(x, d, 0))
                for x, unit in zip(matrix, (1.0, 0.0, 0.0, 1.0))
            ]
            carried = jnp.where(low, 0.0, pltpu.roll(exponent, d, 0))
            matrix, exponent = product(matrix, before, exponent + carried)
        if b == 0:
            x, e = (jnp.broadcast_to(v, shape) for v in log_starts[s])
            y = zero
        whole = [jnp.broadcast_to(v[7:8], shape) for v in matrix]
        whole_e = jnp.broadcast_to(exponent[7:8], shape)
        for k in range(parts - 1, 0, -1):
            here = part >= k
            t00, t01, t10, t11, te = (pltpu.roll(v, k * cycles, 1) for v in whole + [whole_e])
            (x2, y2), e2 = rescaled([t00 * x + t01 * y, t10 * x + t11 * y], e + te)
            x, y, e = jnp.where(here, x2, x), jnp.where(here, y2, y), jnp.where(here, e2, e)
        low = sub < 1
        s00, s01, s10, s11 = (
            jnp.where(low, unit, pltpu.roll(v, 1, 0))
            for v, unit in zip(matrix, (1.0, 0.0, 0.0, 1.0))
        )
        total_e = e + jnp.where(low, 0.0, pltpu.roll(exponent, 1, 0))
        half = jnp.floor(total_e * 0.5)
        scale = jnp.exp2(jnp.clip(half, -126.0, 126.0))
        first = jnp.exp2(jnp.clip(total_e - half, -126.0, 126.0))
        start_x = (s00 * x + s01 * y) * first
        start_y = (s10 * x + s11 * y) * first
        for t in range(STEPS):
            value = (u_ref[j, t] * start_x + v_ref[j, t] * start_y) * scale
            u_ref[j, t] = jnp.where(bases[j] + float(t) >= ms[j], value, 0.0)
        if b < blocks - 1:
            t00, t01, t10, t11 = whole
            (x, y), e = rescaled([t00 * x + t01 * y, t10 * x + t11 * y], e + whole_e)
        stack = LANES // STEPS
        for a in range(8 // stack):
            tall = jnp.concatenate(
                [u_ref[j, :, a * stack + k, :] for k in range(stack)], axis=0
            )
            turned = tall.T
            for g in range(parts):
                at = ((b * parts + g) * 8 + a * stack) * STEPS
                leg_ref[s * cycles : (s + 1) * cycles, at : at + LANES] = turned[
                    g * cycles : (g + 1) * cycles
                ].astype(BF16)


def main_kernel(
    n_ma, n_freq, m_hbm, kept_hbm, cyc_hbm, coef_hbm, vec_hbm, beam_hbm, sum_out, table_out,
    m_ref, kept_ref, cyc_ref, coef, vec, beam, ints, ints_send, part, precv, zsend, zrecv,
    u_ref, v_ref, leg, tab, svd, modes, mrecv,
    small_sem, vec_sem, beam_sem, isend_sem, irecv_sem, dsend_sem, drecv_sem,
    zsend_sem, zrecv_sem, msend_sem, mrecv_sem,
):
    slots, quads, n_modes = coef.shape
    n_groups, _, _, span, depth = vec.shape
    channels, length = beam.shape[1:3]
    n_cyc = cyc_hbm.shape[0]
    cycles = n_cyc * n_ma
    n_z = n_freq // 2
    per_group = n_z // n_groups
    rows = channels * quads
    wide = svd.shape[0]
    ma, fr = lax.axis_index("ma"), lax.axis_index("freq")
    z, core = fr // 2, lax.rem(fr, 2)
    other = 1 - core
    partner = z * 2 + other
    my_group, my_place = z // per_group, lax.rem(z, per_group)

    def reached(x):
        return (x + n_groups) // n_groups

    upper = reached(2 * my_group - n_groups)

    def group_at(o):
        if o == n_groups - 1:
            return my_group
        low = n_groups - 1 - o
        return upper * (o + reached(o - my_group)) + (1 - upper) * (low - reached(my_group - low))

    smalls = [
        pltpu.make_async_copy(src, dst, small_sem.at[i])
        for i, (src, dst) in enumerate(
            [(coef_hbm, coef), (kept_hbm, kept_ref), (m_hbm, m_ref), (cyc_hbm, cyc_ref)]
        )
    ]
    for copy in smalls:
        copy.start()
    vec_copies = [
        [
            pltpu.make_async_copy(
                vec_hbm.at[s, :, pl.ds(pl.multiple_of(group_at(o) * span, span), span), :],
                vec.at[o, s], vec_sem.at[o, s],
            )
            for s in range(slots)
        ]
        for o in range(n_groups)
    ]
    beam_copies = [
        [
            pltpu.make_async_copy(beam_hbm.at[s, c], beam.at[s, c], beam_sem.at[s, c])
            for c in range(channels)
        ]
        for s in range(slots)
    ]
    for pair in vec_copies:
        for copy in pair:
            copy.start()

    barrier = pltpu.get_barrier_semaphore()
    for k in range(1, n_ma):
        pl.semaphore_signal(
            barrier, inc=1, device_id=(lax.rem(ma + k, n_ma), fr), device_id_type=MESH
        )
    for k in range(1, n_z):
        pl.semaphore_signal(
            barrier, inc=1, device_id=(ma, lax.rem(fr + 2 * k, n_freq)), device_id_type=MESH
        )
    pl.semaphore_signal(barrier, inc=1, device_id=(ma, partner), device_id_type=MESH)

    svd[...] = jnp.zeros_like(svd)
    flat_wide = n_modes * span
    row = lax.broadcasted_iota(jnp.int32, (span * quads, flat_wide), 0)
    column = lax.broadcasted_iota(jnp.int32, (span * quads, flat_wide), 1)
    same_channel = row // quads == column % span
    spread = (
        lax.broadcasted_iota(jnp.int32, (n_modes, flat_wide), 1) // span
        == lax.broadcasted_iota(jnp.int32, (n_modes, flat_wide), 0)
    )
    spread = jnp.where(spread, 1.0, 0.0).astype(BF16)
    mode = fr * n_modes + lax.broadcasted_iota(jnp.int32, (quads, n_modes), 1)
    smalls[0].wait()
    smalls[1].wait()
    weights = []
    for s in range(slots):
        masked = jnp.where(mode < kept_ref[s], coef[s].astype(F32), 0.0)
        tall = jnp.concatenate([masked] * span, axis=0).astype(BF16)
        full = jnp.dot(tall, spread, preferred_element_type=F32)
        weights.append(jnp.where(same_channel, full, 0.0).astype(BF16))
    smalls[2].wait()
    smalls[3].wait()
    lane = lax.broadcasted_iota(jnp.int32, (8, LANES), 1)
    line = lax.broadcasted_iota(jnp.int32, (8, LANES), 0)
    packed = jnp.zeros((8, LANES), jnp.int32)
    for i in range(n_cyc):
        here = (line == 0) & (lane % cycles == ma * n_cyc + i)
        packed = jnp.where(here, cyc_ref[i], packed)
    for s in range(slots):
        packed = jnp.where((line == 1) & (lane == ma * slots + s), m_ref[s], packed)
    ints_send[...] = packed

    int_copies, pair_copies = [], []
    for o in range(n_groups):
        for s in range(slots):
            vec_copies[o][s].wait()
            flat = vec[o, s].reshape(flat_wide, depth)
            value = jnp.dot(weights[s], flat, preferred_element_type=F32).astype(BF16)
            for j in range(per_group):
                for k in range(2):
                    at = (j * 2 + k) * rows
                    part[o, k, j, s] = value[at : at + rows]
        if o == 0:
            pl.semaphore_wait(barrier, n_ma - 1 + n_z - 1 + 1)
        copy = pltpu.make_async_remote_copy(
            src_ref=part.at[o, other], dst_ref=precv.at[o], send_sem=dsend_sem.at[o],
            recv_sem=drecv_sem.at[o], device_id=(ma, partner), device_id_type=MESH,
        )
        copy.start()
        pair_copies.append(copy)
        if o == 0:
            for k in range(1, n_ma):
                copy = pltpu.make_async_remote_copy(
                    src_ref=ints_send, dst_ref=ints.at[k], send_sem=isend_sem.at[k],
                    recv_sem=irecv_sem.at[k], device_id=(lax.rem(ma + k, n_ma), fr),
                    device_id_type=MESH,
                )
                copy.start()
                int_copies.append(copy)
            for group in beam_copies:
                for copy in group:
                    copy.start()

    z_copies = []
    for o in range(n_groups):
        pair_copies[o].wait_recv()
        joined = part[o, core].astype(F32) + precv[o].astype(F32)
        zsend[o] = joined.astype(BF16)
        for step in range(1 if o == n_groups - 1 else 0, per_group):
            j = lax.rem(my_place + step, per_group)
            to = group_at(o) * per_group + j
            k = lax.rem(to - z + n_z, n_z)
            copy = pltpu.make_async_remote_copy(
                src_ref=zsend.at[o, j], dst_ref=zrecv.at[k],
                send_sem=zsend_sem.at[o, step], recv_sem=zrecv_sem.at[k],
                device_id=(ma, to * 2 + core), device_id_type=MESH,
            )
            copy.start()
            z_copies.append(copy)

    for copy in int_copies:
        copy.wait_recv()
    for k in range(1, n_ma):
        packed = packed + ints[k]
    cos_theta, sin_theta = cycle_angles(packed[0:1])
    m_values = [m_ref[s].astype(F32) for s in range(slots)]
    legendre_into(m_values, cos_theta, sin_theta, cycles, length, u_ref, v_ref, leg)
    for s in range(slots):
        for c in range(channels):
            beam_copies[s][c].wait()
            value = jnp.dot(
                leg[s * cycles : (s + 1) * cycles, :], beam[s, c], preferred_element_type=F32
            )
            at = (s * channels + c) * cycles
            tab[at : at + cycles] = value.astype(BF16)

    n_lines = n_ma * slots * 2
    line = lax.broadcasted_iota(jnp.int32, (n_lines, LANES), 0)
    lane = lax.broadcasted_iota(jnp.int32, (n_lines, LANES), 1)
    m_all = jnp.broadcast_to(packed[1:2].astype(F32), (n_lines, LANES))
    m_column = jnp.sum(jnp.where(lane == line // 2, m_all, 0.0), axis=1, keepdims=True)
    line = lax.broadcasted_iota(jnp.int32, (n_lines, NPHI), 0)
    time = lax.broadcasted_iota(jnp.int32, (n_lines, NPHI), 1)
    m = jnp.broadcast_to(m_column.astype(jnp.int32), (n_lines, NPHI))
    table = turn_cosine(m * time + (line % 2) * (NPHI // 4))
    table = (jnp.where(m == 0, 1.0, 2.0) * table).astype(BF16)
    to_row = lax.broadcasted_iota(jnp.int32, (wide, n_lines), 0)
    from_row = lax.broadcasted_iota(jnp.int32, (wide, n_lines), 1)
    pick = to_row // (quads * channels) * 2 + to_row % 2 == from_row
    pick = jnp.where(pick, 1.0, 0.0).astype(BF16)
    table_out[...] = jnp.dot(pick, table, preferred_element_type=F32).astype(BF16)

    total = zsend[n_groups - 1, my_place].astype(F32)
    for k in range(1, n_z):
        pltpu.make_async_remote_copy(
            src_ref=zsend.at[0, 0], dst_ref=zrecv.at[k], send_sem=zsend_sem.at[0, 0],
            recv_sem=zrecv_sem.at[k], device_id=(ma, fr), device_id_type=MESH,
        ).wait_recv()
        total = total + zrecv[k].astype(F32)
    mine = slots * rows
    svd[pl.ds(pl.multiple_of(ma * mine, mine), mine), :] = total.reshape(mine, depth).astype(BF16)
    every = lax.dot_general(
        tab[...], svd[...], (((1,), (1,)), ((), ())), preferred_element_type=F32
    )
    lane = lax.broadcasted_iota(jnp.int32, (cycles, wide), 1)
    owner = lane // quads % (slots * channels)
    chosen = jnp.zeros((cycles, wide), F32)
    for i in range(slots * channels):
        chosen = jnp.where(owner == i, every[i * cycles : (i + 1) * cycles], chosen)
    modes[...] = chosen.reshape(n_ma, n_cyc, wide)
    mode_copies = []
    for k in range(1, n_ma):
        to = lax.rem(ma + k, n_ma)
        copy = pltpu.make_async_remote_copy(
            src_ref=modes.at[to], dst_ref=mrecv.at[k], send_sem=msend_sem.at[k],
            recv_sem=mrecv_sem.at[k], device_id=(to, fr), device_id_type=MESH,
        )
        copy.start()
        mode_copies.append(copy)
    for copy in int_copies + pair_copies + z_copies:
        copy.wait_send()
    gathered = modes[ma]
    for copy in mode_copies:
        copy.wait_recv()
    for k in range(1, n_ma):
        gathered = gathered + mrecv[k]
    sum_out[...] = gathered
    for copy in mode_copies:
        copy.wait_send()


def main_call(n_ma, n_freq, m_table, retained_modes, cycle_ids, kl_coeffs, kl_vectors, beam):
    slots, quads, n_modes = kl_coeffs.shape
    all_channels, depth = kl_vectors.shape[2:]
    channels, length = beam.shape[1:3]
    n_cyc = cycle_ids.shape[0]
    cycles = n_cyc * n_ma
    n_z = n_freq // 2
    span = max(8, 2 * channels)
    n_groups = all_channels // span
    per_group = n_z // n_groups
    rows = channels * quads
    wide = max(LANES, n_ma * slots * rows)
    blocks = slots * length // (STEPS * 8 * (LANES // cycles))
    held = (m_table, retained_modes, cycle_ids, kl_coeffs, kl_vectors, beam)
    hbm = pl.BlockSpec(memory_space=pltpu.HBM)
    vmem = pl.BlockSpec(memory_space=pltpu.VMEM)
    dma = pltpu.SemaphoreType.DMA
    return pl.pallas_call(
        functools.partial(main_kernel, n_ma, n_freq),
        out_shape=(
            jax.ShapeDtypeStruct((n_cyc, wide), F32),
            jax.ShapeDtypeStruct((wide, NPHI), BF16),
        ),
        in_specs=[hbm] * 6,
        out_specs=(vmem, vmem),
        scratch_shapes=[
            pltpu.SMEM((slots,), jnp.int32),
            pltpu.SMEM((slots,), jnp.int32),
            pltpu.SMEM((n_cyc,), jnp.int32),
            pltpu.VMEM(kl_coeffs.shape, BF16),
            pltpu.VMEM((n_groups, slots, n_modes, span, depth), BF16),
            pltpu.VMEM(beam.shape, BF16),
            pltpu.VMEM((n_ma, 8, LANES), jnp.int32),
            pltpu.VMEM((8, LANES), jnp.int32),
            pltpu.VMEM((n_groups, 2, per_group, slots, rows, depth), BF16),
            pltpu.VMEM((n_groups, per_group, slots, rows, depth), BF16),
            pltpu.VMEM((n_groups, per_group, slots, rows, depth), BF16),
            pltpu.VMEM((n_z, slots, rows, depth), BF16),
            pltpu.VMEM((blocks, STEPS, 8, LANES), F32),
            pltpu.VMEM((blocks, STEPS, 8, LANES), F32),
            pltpu.VMEM((slots * cycles, length), BF16),
            pltpu.VMEM((slots * channels * cycles, depth), BF16),
            pltpu.VMEM((wide, depth), BF16),
            pltpu.VMEM((n_ma, n_cyc, wide), F32),
            pltpu.VMEM((n_ma, n_cyc, wide), F32),
            dma((4,)),
            dma((n_groups, slots)),
            dma((slots, channels)),
            dma((n_ma,)),
            dma((n_ma,)),
            dma((n_groups,)),
            dma((n_groups,)),
            dma((n_groups, per_group)),
            dma((n_z,)),
            dma((n_ma,)),
            dma((n_ma,)),
        ],
        compiler_params=pltpu.CompilerParams(
            collective_id=0, has_side_effects=True, vmem_limit_bytes=32 * 2**20
        ),
        name="cycle_modes",
    )(*[pltpu.with_memory_space_constraint(x, pltpu.HBM) for x in held])


def sky_kernel(channels, sum_ref, table_ref, out_hbm, out, sem):
    n_cyc, wide = sum_ref.shape
    pieces, step = out.shape[0], out.shape[4]
    rows = n_cyc * 2 * channels
    row = lax.broadcasted_iota(jnp.int32, (rows, wide), 0)
    lane = lax.broadcasted_iota(jnp.int32, (rows, wide), 1)
    wanted = (lane // 4 % channels == row % channels) & (lane % 4 // 2 == row // channels % 2)
    spread = jnp.broadcast_to(sum_ref[...][:, None, :], (n_cyc, 2 * channels, wide))
    left = jnp.where(wanted, spread.reshape(rows, wide), 0.0).astype(BF16)
    copies = []
    for i in range(pieces):
        value = jnp.dot(
            left, table_ref[:, i * step : (i + 1) * step], preferred_element_type=F32
        )
        for r in range(n_cyc * 2):
            out[i, r // 2, r % 2] = value[r * channels : (r + 1) * channels]
        copy = pltpu.make_async_copy(
            out.at[i], out_hbm.at[:, :, :, pl.ds(i * step, step)], sem.at[i]
        )
        copy.start()
        copies.append(copy)
    for copy in copies:
        copy.wait()


def sky_call(channels, gathered, table):
    n_cyc = gathered.shape[0]
    pieces = 4
    return pl.pallas_call(
        functools.partial(sky_kernel, channels),
        out_shape=jax.ShapeDtypeStruct((n_cyc, 2, channels, NPHI), F32),
        in_specs=[pl.BlockSpec(memory_space=pltpu.VMEM)] * 2,
        out_specs=pl.BlockSpec(memory_space=pltpu.HBM),
        scratch_shapes=[
            pltpu.VMEM((pieces, n_cyc, 2, channels, NPHI // pieces), F32),
            pltpu.SemaphoreType.DMA((pieces,)),
        ],
        compiler_params=pltpu.CompilerParams(vmem_limit_bytes=16 * 2**20),
        name="sky_maps",
    )(gathered, table)


def local(n_ma, n_freq, m_table, retained_modes, cycle_ids, kl_coeffs, kl_vectors, beam_matrix):
    gathered, table = main_call(
        n_ma, n_freq, m_table, retained_modes, cycle_ids, kl_coeffs, kl_vectors, beam_matrix
    )
    return sky_call(beam_matrix.shape[1], gathered, table)


def solution(mesh):
    placed = (
        P("ma"),
        P("ma"),
        P("ma"),
        P("ma", None, "freq"),
        P("ma", "freq", None, None),
        P("ma", "freq", None, None),
    )
    return jax.shard_map(
        functools.partial(local, mesh.shape["ma"], mesh.shape["freq"]),
        mesh=mesh, in_specs=placed, out_specs=P("ma", None, "freq", None), check_vma=False,
    )
```

time: 32.8 us -> 16.5 us (0.50)
  Pallas kernels: 30.5 us -> 16.4 us
  local copies, waits for them, and re-layouts: 1.98 us -> 0 us
    pallas_call x3 -> x2, Pallas kernels: 30.5 us -> 16.4 us  [the longest x1 15.4 us: main_call(): pl.pallas_call(functools.partial(main_kernel, n_ma, n_freq), out_shape=(j...]
    reshape x1 -> x0, local copies, waits for them, and re-layouts: 1.98 us -> none  [local(): return sky.reshape(n_cyc, 2, channels, NPHI)]
where the time goes in v1:
time: 16.5 us; the launch traced here: 16.4 us
  Pallas kernels  16.4 us (99%)
    pallas_call x1, Pallas kernels, main_call(): pl.pallas_call(functools.partial(main_kernel, n_ma, n_freq), out_shape=(j...  15.4 us
    pallas_call x1, Pallas kernels, sky_call(): pl.pallas_call(functools.partial(sky_kernel, channels), out_shape=jax.Sha...  0.98 us

profile of v1, /device:TPU:0, one launch (start us, length us, event | category | flops | bytes accessed | tf_op | source)
XLA Modules:
  0.0 16.4 jit_solution(3795058784186538649)
XLA Ops:
  0.0 15.4 %cycle_modes.1 = (f32[8,128]{1,0:T(8,128)S(1)}, bf16[128,2048]{1,0:T(8,128)(2,1)S(1)}) custom-call(s32[2]{0:T(128)} %m_hbm.1, s32[2]{0:T(128)} %kept_hbm.1, s32[8]{0:T(128)} %cyc_hbm.1, bf16[2,4,64]{2,1,0:T(4,128)(2,1)} %coef_hbm.1, bf16[2,64,32,512]{3,2,1,0:T(8,128)(2,1)} %vec_hbm.1, bf16[2,4,1024,512]{3,2,1,0:T(8,128)(2,1)} %beam_hbm.1), custom_call_target="tpu_custom_call" | custom-call | tf_op jit(solution)/shard_map/cycle_modes/pallas_call | solution.py:420
  15.4 1.0 %sky_maps.1 = f32[8,2,4,2048]{3,2,1,0:T(4,128)} custom-call(f32[8,128]{1,0:T(8,128)S(1)} %get-tuple-element.7.sum_ref, bf16[128,2048]{1,0:T(8,128)(2,1)S(1)} %get-tuple-element.8.table_ref), custom_call_target="tpu_custom_call" | custom-call | tf_op jit(solution)/shard_map/sky_maps/pallas_call | solution.py:495
